TPU v7x, 32 devices: a whole 2x2x4 slice. The times are simulated.
32 devices in a mesh: row: 4 (over y, core), col: 8 (over z, x).
Axes of the slice: x: 2, y: 2, z: 4, core: 2. Of those that a mesh axis runs over, the one named last changes fastest.
Arguments:
- factor: float32 [6, 2048, 6, 2048], P(None, 'row', None, 'col'), may hold values from -0.0625 to 0.0625
- diag_inv: float32 [6, 2048, 2048], P(None, None, 'row'), may hold values from -2 to 2, as said below
- structure: int32 [6, 6, 16], P(None, None, 'row'), may hold values 0 or 1
- parent: int32 [6], replicated, may hold values from 1 to 6, as said below
- post: float32 [6, 2048, 64], P(None, 'row', 'col'), may hold values from -6 to 6
Outputs:
- mean_x: float32 [6, 2048, 64], P(None, 'row', 'col')
- variance: float32 [6, 2048], P(None, 'row')
Inputs may be any that keep to these rules, and one draw needn't show every extreme that they name: parent[s] > s for s < 5, and parent[5] = 6; every supernode has at most 2 ancestors, and some supernode has exactly that many. The diagonal of each diag_inv[s] lies in 0.5 to 2.
All inputs are finite; a program needn't handle non-finite values. No bound on the sum of `structure` on one device may be relied on, other than what follows from the above.
Results may differ from a plain program's by a relative error of at most 0.00014.
Values sent between devices are 32-bit elements; how exact they have to be, the bound alone decides.
A program may use at most 192 MiB of HBM per device.

v0:
```python
import jax
import jax.numpy as jnp
from jax import lax
from jax.sharding import PartitionSpec as P

HIGH = lax.Precision.HIGH


def product(left, right):
    return jnp.dot(left, right, precision=HIGH, preferred_element_type=jnp.float32)


def body(factor, diag_inv, structure, parent, post):
    super_count = factor.shape[0]
    row_width = factor.shape[1]
    col_width = factor.shape[3]
    full_width = diag_inv.shape[1]
    row_at = lax.axis_index("row")
    col_at = lax.axis_index("col")
    last = super_count - 1
    block_rows = row_width // structure.shape[2]

    extended = jnp.concatenate([parent, jnp.full((1,), super_count, jnp.int32)])
    first_at = parent
    second_at = extended[parent]

    def pick(current_sup, target):
        clamped = jnp.minimum(target, last)
        block = lax.dynamic_index_in_dim(factor[:, :, current_sup, :], clamped, 0, keepdims=False)
        flags = lax.dynamic_index_in_dim(structure[current_sup], clamped, 0, keepdims=False)
        flags = jnp.where(target < super_count, flags.astype(jnp.float32), 0.0)
        return block * jnp.repeat(flags, block_rows)[:, None]

    blocks = [None] * super_count
    for current_sup in range(last - 1, -1, -1):
        mine = jnp.concatenate(
            [pick(current_sup, first_at[current_sup]), pick(current_sup, second_at[current_sup])], axis=0
        )
        blocks[current_sup] = lax.all_gather(mine, "col", axis=1, tiled=True)

    own_cols = row_at * row_width + jnp.arange(row_width, dtype=jnp.int32)
    rows_full = jnp.arange(full_width, dtype=jnp.int32)
    keep = rows_full[:, None] >= own_cols[None, :]
    lower = [jnp.where(keep, diag_inv[s], 0.0) for s in range(super_count)]
    unit_rows = col_at * col_width + jnp.arange(col_width, dtype=jnp.int32)
    own = lax.dynamic_slice_in_dim(diag_inv, col_at * col_width, col_width, axis=1)
    own = jnp.where((unit_rows[:, None] >= own_cols[None, :])[None], own, 0.0)
    gathered = jnp.swapaxes(lax.all_gather(post, "row", axis=1, tiled=True), 1, 2)

    def take(stacked, target):
        return lax.dynamic_index_in_dim(stacked, jnp.minimum(target, last), 0, keepdims=False)

    rhs = jnp.stack([product(gathered[s], lower[s]) for s in range(super_count)])

    def solve(current_sup, unit_part, rhs_part):
        summed = lax.psum(jnp.concatenate([unit_part, rhs_part], axis=0), "row")
        right = jnp.concatenate(
            [-summed[:col_width], gathered[current_sup] - summed[col_width:]], axis=0
        )
        fresh = product(right, lower[current_sup])
        return fresh[:col_width], fresh[col_width:]

    near = [jnp.zeros((col_width, row_width), jnp.float32)] * super_count
    means = [rhs[s] for s in range(super_count)]
    for s in range(last - 1, -1, -1):
        one, two = first_at[s], second_at[s]
        unit_part = product(take(own, one), blocks[s][:row_width])
        rhs_part = product(
            jnp.concatenate([take(rhs, one), take(rhs, two)], axis=1), blocks[s]
        )
        near[s], means[s] = solve(s, unit_part, rhs_part)
    near_all = jnp.stack(near)
    rhs = jnp.stack(means)

    far = [None] * super_count
    for s in range(last - 1, -1, -1):
        one, two = first_at[s], second_at[s]
        selected = jnp.concatenate(
            [
                jnp.concatenate([take(near_all, one), take(own, two)], axis=1),
                jnp.concatenate([take(rhs, one), take(rhs, two)], axis=1),
            ],
            axis=0,
        )
        both = product(selected, blocks[s])
        far[s], means[s] = solve(s, both[:col_width], both[col_width:])

    squares = []
    for s in range(super_count):
        total = jnp.sum(own[s] * own[s], axis=0)
        if s < last:
            total = total + jnp.sum(near[s] * near[s], axis=0) + jnp.sum(far[s] * far[s], axis=0)
        squares.append(total)
    variance = lax.psum(jnp.stack(squares), "col")
    mean_x = jnp.swapaxes(jnp.stack(means), 1, 2)
    return (mean_x, variance)


def solution(mesh):
    return jax.shard_map(
        body,
        mesh=mesh,
        in_specs=(
            P(None, "row", None, "col"),
            P(None, None, "row"),
            P(None, None, "row"),
            P(),
            P(None, "row", "col"),
        ),
        out_specs=(P(None, "row", "col"), P(None, "row")),
        check_vma=False,
    )
```

profile of v0, /device:TPU:10, one launch (start us, length us, event | category | flops | bytes accessed | tf_op | source)
XLA Modules:
  0.0 1181.0 jit_solution(15968273963925713293)
XLA Ops:
  7.9 1.5 fusion.293
  17.9 11.0 fusion.291
  28.9 2.9 bitcast_multiply_fusion.5
  31.7 1.0 pad_maximum_fusion.6
  32.9 2.2 pad_maximum_fusion.7
  41.1 3.1 bitcast_multiply_fusion.1
  44.2 1.1 pad_maximum_fusion.8
  45.4 2.3 pad_maximum_fusion.9
  50.5 1.1 pad_maximum_fusion.5
  51.7 7.2 all_gather.19
  58.9 3.5 fusion.109
  62.5 3.5 fusion.115
  66.0 3.6 fusion.121
  69.6 3.6 fusion.127
  73.2 3.5 fusion.133
  76.7 3.5 constant_dynamic-update-slice_fusion
  81.1 2.4 dynamic-slice_select_fusion
  83.4 73.0 %all-gather.8.cloned.1.call-done = f32[1024,2048]{1,0:T(8,128)} async-done(((f32[1024,256]{1,0:T(8,128)}), f32[1024,2048]{1,0:T(8,128)}) %all-gather.8.cloned.1.call-update) | async-done | bytes 8388624 | tf_op jit(solution)/shard_map/all_gather | solution.py:39
  156.4 4.2 fusion.6
  160.7 5.7 fusion.204
  166.4 1.6 pad_maximum_fusion.1
  167.9 113.7 %all-gather.10.cloned.1.call-done = f32[1024,2048]{1,0:T(8,128)} async-done(((f32[1024,256]{1,0:T(8,128)}), f32[1024,2048]{1,0:T(8,128)}) %all-gather.10.cloned.1.call-update) | async-done | bytes 8388624 | tf_op jit(solution)/shard_map/all_gather | solution.py:39
  281.6 4.2 fusion.4
  285.9 5.5 fusion.208
  291.4 1.5 pad_maximum_fusion.2
  292.9 113.9 %all-gather.12.cloned.1.call-done = f32[1024,2048]{1,0:T(8,128)} async-done(((f32[1024,256]{1,0:T(8,128)}), f32[1024,2048]{1,0:T(8,128)}) %all-gather.12.cloned.1.call-update) | async-done | bytes 8388624 | tf_op jit(solution)/shard_map/all_gather | solution.py:39
  406.8 4.2 fusion.2
  411.1 5.5 fusion.212
  416.6 1.5 pad_maximum_fusion.3
  418.1 113.8 %all-gather.14.cloned.1.call-done = f32[1024,2048]{1,0:T(8,128)} async-done(((f32[1024,256]{1,0:T(8,128)}), f32[1024,2048]{1,0:T(8,128)}) %all-gather.14.cloned.1.call-update) | async-done | bytes 8388624 | tf_op jit(solution)/shard_map/all_gather | solution.py:39
  531.9 4.2 fusion
  536.1 5.9 fusion.216
  542.0 1.5 pad_maximum_fusion.4
  543.5 113.4 %all-gather.6.cloned.1.call-done = f32[1024,2048]{1,0:T(8,128)} async-done(((f32[1024,256]{1,0:T(8,128)}), f32[1024,2048]{1,0:T(8,128)}) %all-gather.6.cloned.1.call-update) | async-done | bytes 8388624 | tf_op jit(solution)/shard_map/all_gather | solution.py:39
  656.9 4.2 fusion.8
  661.2 5.5 fusion.200
  666.7 1.5 pad_maximum_fusion
  668.3 2.4 fusion.179
  670.7 190.8 %all-reduce.7.cloned.1.call-done = (f32[264,2048]{1,0:T(8,128)}, f32[264,2048]{1,0:T(8,128)}, f32[264,2048]{1,0:T(8,128)}, f32[264,2048]{1,0:T(8,128)}, f32[264,2048]{1,0:T(8,128)}) async-done(((f32[264,2048]{1,0:T(8,128)}, f32[264,2048]{1,0:T(8,128)}, f32[264,2048]{1,0:T(8,128)}, f32[264,2048]{1,0:T(8,128)}, f32[264,2048]{1,0:T(8,128)}), (f32[264,2048]{1,0:T(8,128)}, f32[264,2048]{1,0:T(8,128)}, ...) | async-done | bytes 10813456 | tf_op jit(solution)/shard_map/psum | solution.py:56
  861.5 2.0 slice_negate_fusion.9
  864.0 1.2 copy-done.2
  866.1 1.0 copy-done
  867.2 0.9 slice_subtract_fusion.5
  868.3 4.2 fusion.35
  872.6 4.3 fusion.37
  876.9 4.3 fusion.39
  881.1 4.3 fusion.41
  885.4 4.4 fusion.43
  890.4 1.7 slice-done.9
  892.3 6.0 fusion.139
  898.3 5.8 fusion.147
  904.2 5.8 fusion.155
  910.1 6.1 fusion.163
  916.1 5.8 fusion.171
  922.3 192.2 %all-reduce.5.cloned.1.call-done = (f32[264,2048]{1,0:T(8,128)}, f32[264,2048]{1,0:T(8,128)}, f32[264,2048]{1,0:T(8,128)}, f32[264,2048]{1,0:T(8,128)}, f32[264,2048]{1,0:T(8,128)}) async-done(((f32[264,2048]{1,0:T(8,128)}, f32[264,2048]{1,0:T(8,128)}, f32[264,2048]{1,0:T(8,128)}, f32[264,2048]{1,0:T(8,128)}, f32[264,2048]{1,0:T(8,128)}), (f32[264,2048]{1,0:T(8,128)}, f32[264,2048]{1,0:T(8,128)}, ...) | async-done | bytes 10813456 | tf_op jit(solution)/shard_map/psum | solution.py:56
  1114.5 1.9 slice_negate_fusion.4
  1117.0 1.1 copy-done.6
  1119.0 1.0 copy-done.4
  1121.1 4.3 fusion.34
  1125.4 4.5 fusion.42
  1130.1 4.3 fusion.40
  1134.4 4.3 fusion.38
  1138.8 4.3 fusion.36
  1143.3 30.5 %psum.87 = f32[6,512]{1,0:T(8,128)} all-reduce(f32[6,512]{1,0:T(8,128)S(1)} %stack.112), channel_id=1, replica_groups=mesh['row'=4,'col'=8] {'col'}, use_global_device_ids=true, to_apply=%region_26.27 | all-reduce | flops 3072 | bytes 24576 | tf_op jit(solution)/shard_map/psum | solution.py:94
  (168 shorter events, 12.2 us)
Async XLA Ops:
  7.2 149.3 %all-gather.8.cloned.1.call-start = ((), (), s32[]{:S(2)}) async-start(), calls=%async_computation.1 | async-start | bytes 9437184 | tf_op jit(solution)/shard_map/all_gather | solution.py:39
  32.8 248.8 %all-gather.10.cloned.1.call-start = ((), (), s32[]{:S(2)}) async-start(), calls=%async_computation.2 | async-start | bytes 9437184 | tf_op jit(solution)/shard_map/all_gather | solution.py:39
  35.1 371.7 %all-gather.12.cloned.1.call-start = ((), (), s32[]{:S(2)}) async-start(), calls=%async_computation.3 | async-start | bytes 9437184 | tf_op jit(solution)/shard_map/all_gather | solution.py:39
  45.3 486.5 %all-gather.14.cloned.1.call-start = ((), (), s32[]{:S(2)}) async-start(), calls=%async_computation.4 | async-start | bytes 9437184 | tf_op jit(solution)/shard_map/all_gather | solution.py:39
  47.7 609.2 %all-gather.6.cloned.1.call-start = ((), (), s32[]{:S(2)}) async-start(), calls=%async_computation | async-start | bytes 9437184 | tf_op jit(solution)/shard_map/all_gather | solution.py:39
  51.6 809.9 %all-reduce.7.cloned.1.call-start = ((), (), s32[]{:S(2)}) async-start(), calls=%async_computation.6 | async-start | bytes 21626880 | tf_op jit(solution)/shard_map/psum | solution.py:56
  51.7 29.2 %copy-start.13 = (s32[512]{0:T(512)}, s32[512]{0:T(512)S(1)}, u32[]{:S(2)}) copy-start(s32[512]{0:T(512)S(1)} %iota_add_fusion) | copy-start | bytes 6148
  156.4 4.2 copy-start.23
  156.4 4.2 copy-start.24
  281.6 4.2 copy-start.21
  281.6 4.2 copy-start.22
  406.8 4.2 copy-start.19
  406.8 4.2 copy-start.20
  531.9 4.2 copy-start.17
  531.9 4.2 copy-start.18
  656.9 4.2 copy-start.15
  656.9 4.2 copy-start.16
  668.3 446.2 %all-reduce.5.cloned.1.call-start = ((), (), s32[]{:S(2)}) async-start(), calls=%async_computation.5 | async-start | bytes 21626880 | tf_op jit(solution)/shard_map/psum | solution.py:56
  861.5 2.2 copy-start.1
  863.5 1.7 copy-start.2
  864.0 1.9 copy-start.3
  865.4 1.7 copy-start
  866.1 2.2 copy-start.14
  885.4 5.0 slice-start.8
  889.9 2.2 slice-start.9
  890.1 2.2 copy-start.12
  890.2 8.1 slice-start
  892.3 6.0 slice-start.1
  892.3 6.0 copy-start.11
  892.3 11.9 %slice-start.2 = ((s8[8388608]{0:T(1024)(128)(4,1)}), s8[4194304]{0:T(1024)(128)(4,1)S(1)}, s32[]{:S(2)}) async-start(s8[8388608]{0:T(1024)(128)(4,1)} %bitcast.341), calls=%async_computation.9 | async-start | bytes 8388608
  898.3 5.9 slice-start.3
  898.3 5.9 copy-start.10
  898.3 11.7 slice-start.4
  904.2 5.9 slice-start.5
  904.2 5.9 copy-start.9
  904.2 11.9 %slice-start.6 = ((s8[8388608]{0:T(1024)(128)(4,1)}), s8[4194304]{0:T(1024)(128)(4,1)S(1)}, s32[]{:S(2)}) async-start(s8[8388608]{0:T(1024)(128)(4,1)} %bitcast.345), calls=%async_computation.13 | async-start | bytes 8388608
  910.0 6.1 slice-start.7
  910.0 6.1 copy-start.8
  1114.5 2.2 copy-start.5
  1116.4 1.7 copy-start.6
  1116.9 1.8 copy-start.7
  1118.3 1.7 copy-start.4
  1138.7 4.5 copy-start.30
  1138.7 4.5 copy-start.29
  1138.7 4.5 copy-start.28
  1138.7 4.5 copy-start.27
  1138.8 4.5 copy-start.26
  1138.8 4.5 copy-start.25
  1143.2 30.7 %copy-start.31 = (f32[6,8,512]{2,1,0:T(8,128)}, f32[6,8,512]{2,1,0:T(8,128)S(1)}, u32[]{:S(2)}) copy-start(f32[6,8,512]{2,1,0:T(8,128)S(1)} %constant_dynamic-update-slice_fusion.7) | copy-start | bytes 294916
Sparse Core Ops, SparseCore 0:
  32.9 123.4 all-gather.7
  158.5 123.1 all-gather.9
  283.7 123.1 all-gather.11
  408.7 123.1 all-gather.13
  533.8 123.1 all-gather.5
  668.4 193.1 all-reduce.6
  922.1 192.3 all-reduce.4
where the time goes:
time: 1190 us; the launch traced here: 1180 us
  waiting for transfers between devices  911 us (77%)
  matrix products  143 us (12%)
  blocking collectives  37.8 us (3%)
  other arithmetic  36.9 us (3%)
  between operations  27.8 us (2%)
  local copies, waits for them, and re-layouts  24.2 us (2%)
    all_gather x5, waiting for transfers between devices, body(): blocks[current_sup] = lax.all_gather(mine, 'col', axis=1, tiled=True)  528 us
    psum x2, waiting for transfers between devices, solve(): summed = lax.psum(jnp.concatenate([unit_part, rhs_part], axis=0), 'row')  383 us
    dot_general x31, matrix products, product(): jnp.dot(left, right, precision=HIGH, preferred_element_type=jnp.float32)  143 us
    psum x1, blocking collectives, body(): variance = lax.psum(jnp.stack(squares), 'col')  30.5 us
  transfers between devices with their start and end apart: 7, of which 7 were waited for; matrix products, arithmetic and copies ran while one was open for 7% of the time, Pallas kernels for 0%

commit v1 on v0

--- a/solution.py
+++ b/solution.py
@@ -1,9 +1,20 @@
+import functools
+
 import jax
 import jax.numpy as jnp
 from jax import lax
+from jax.experimental import pallas as pl
+from jax.experimental.pallas import tpu as pltpu
 from jax.sharding import PartitionSpec as P
 
 HIGH = lax.Precision.HIGH
+MESH = pl.DeviceIdType.MESH
+F32 = jnp.float32
+BF16 = jnp.bfloat16
+VMEM = pltpu.VMEM
+VMEM_LIMIT = 64 * 1000 * 1024
+CORES = 2
+WIDE = 2
 
 
 def product(left, right):
@@ -96,9 +107,609 @@
     return (mean_x, variance)
 
 
+def split(x):
+    high = x.astype(BF16)
+    return high, (x - high.astype(F32)).astype(BF16)
+
+
+def triple(a, b):
+    dot = functools.partial(jnp.dot, preferred_element_type=F32)
+    return dot(a[0], b[0]) + (dot(a[0], b[1]) + dot(a[1], b[0]))
+
+
+def triangle(block, row_start, col_start):
+    rows = lax.broadcasted_iota(jnp.int32, block.shape, 0) + row_start
+    cols = lax.broadcasted_iota(jnp.int32, block.shape, 1) + col_start
+    return jnp.where(rows >= cols, block, 0.0)
+
+
+def near_partial(targets, diag_inv, blocks):
+    count, depth, width = blocks.shape
+    full = diag_inv.shape[1]
+    parts = full // depth
+
+    def kernel(at, lower, block, out):
+        row = lax.axis_index("row")
+        right = split(block[0])
+        for i in range(parts):
+            span = pl.ds(i * depth, depth)
+
+            @pl.when(i >= row)
+            def _():
+                left = triangle(lower[0, span], i * depth, row * depth)
+                out[0, span] = triple(split(left), right)
+
+            @pl.when(i < row)
+            def _():
+                out[0, span] = jnp.zeros((depth, width), F32)
+
+    return pl.pallas_call(
+        kernel,
+        grid_spec=pltpu.PrefetchScalarGridSpec(
+            num_scalar_prefetch=1,
+            grid=(count,),
+            in_specs=[
+                pl.BlockSpec((1, full, depth), lambda e, at: (at[e], 0, 0)),
+                pl.BlockSpec((1, depth, width), lambda e, at: (e, 0, 0)),
+            ],
+            out_specs=pl.BlockSpec((1, full, width), lambda e, at: (e, 0, 0)),
+        ),
+        out_shape=jax.ShapeDtypeStruct((count, full, width), F32),
+        compiler_params=pltpu.CompilerParams(vmem_limit_bytes=VMEM_LIMIT),
+        name="near_partial",
+    )(targets, diag_inv, blocks)
+
+
+def far_partial(slots, targets, valid, near_all, diag_inv, first, second):
+    count, depth, width = second.shape
+    full = diag_inv.shape[1]
+    parts = full // depth
+    cols = near_all.shape[0]
+    share = depth // cols
+
+    def kernel(slot, at, ok, near, lower, one, two, out):
+        e = pl.program_id(0)
+        row = lax.axis_index("row")
+        left_one = split(jnp.where(ok[e] > 0, one[0], 0.0))
+        left_two = split(two[0])
+        for i in range(parts):
+            span = pl.ds(i * depth, depth)
+            rows = near[:, 0, pl.ds(i * share, share)].reshape(depth, depth)
+            out[0, span] = triple(split(rows), left_one)
+
+            @pl.when(i >= row)
+            def _():
+                left = triangle(lower[0, span], i * depth, row * depth)
+                out[0, span] += triple(split(left), left_two)
+
+    return pl.pallas_call(
+        kernel,
+        grid_spec=pltpu.PrefetchScalarGridSpec(
+            num_scalar_prefetch=3,
+            grid=(count,),
+            in_specs=[
+                pl.BlockSpec((cols, 1, parts * share, depth), lambda e, slot, at, ok: (0, slot[e], 0, 0)),
+                pl.BlockSpec((1, full, depth), lambda e, slot, at, ok: (at[e], 0, 0)),
+                pl.BlockSpec((1, depth, width), lambda e, slot, at, ok: (e, 0, 0)),
+                pl.BlockSpec((1, depth, width), lambda e, slot, at, ok: (e, 0, 0)),
+            ],
+            out_specs=pl.BlockSpec((1, full, width), lambda e, slot, at, ok: (e, 0, 0)),
+        ),
+        out_shape=jax.ShapeDtypeStruct((count, full, width), F32),
+        compiler_params=pltpu.CompilerParams(vmem_limit_bytes=VMEM_LIMIT),
+        name="far_partial",
+    )(slots, targets, valid, near_all, diag_inv, first, second)
+
+
+def apply_lower(sources, targets, gathered, diag_inv, post, own, steps):
+    count, height, full = gathered.shape
+    depth = diag_inv.shape[2]
+    parts = full // depth
+    rhs = post.shape[1]
+    share = height // parts
+    last = count - 1
+
+    def kernel(at, of, left, lower, post_of, post_own, y, mean, square, total):
+        e = pl.program_id(0)
+        row = lax.axis_index("row")
+        col = lax.axis_index("col")
+        mean[0] = jnp.zeros((rhs, depth), F32)
+        square[0] = jnp.zeros((8, depth), F32)
+
+        @pl.when(e < count)
+        def _():
+            total[...] = jnp.zeros_like(total)
+            for j in range(parts):
+                span = pl.ds(j * depth, depth)
+
+                @pl.when(j >= row)
+                def _():
+                    right = triangle(lower[0, span], j * depth, row * depth)
+                    total[...] += triple(split(left[0, :, span]), split(right))
+
+            found = -total[...]
+            y[0] = found
+            mean[0] = triple(split(post_of[0]), split(found))
+            square[0] = jnp.sum((found * found).reshape(height // 8, 8, depth), axis=0)
+
+        if own:
+            for i in range(parts):
+                start = i * depth + col * share
+                mine = triangle(lower[0, pl.ds(pl.multiple_of(start, 8), share)], start, row * depth)
+                total[pl.ds(i * share, share)] = mine
+            found_own = total[...]
+            mean[0] += triple(split(post_own[0]), split(found_own))
+            square[0] += jnp.sum((found_own * found_own).reshape(height // 8, 8, depth), axis=0)
+
+    return pl.pallas_call(
+        kernel,
+        grid_spec=pltpu.PrefetchScalarGridSpec(
+            num_scalar_prefetch=2,
+            grid=(steps,),
+            in_specs=[
+                pl.BlockSpec((1, height, full), lambda e, at, of: (jnp.minimum(e, last), 0, 0)),
+                pl.BlockSpec((1, full, depth), lambda e, at, of: (at[e], 0, 0)),
+                pl.BlockSpec((1, rhs, height), lambda e, at, of: (of[e], 0, 0)),
+                pl.BlockSpec((1, rhs, height), lambda e, at, of: (at[e], 0, 0)),
+            ],
+            out_specs=[
+                pl.BlockSpec((1, height, depth), lambda e, at, of: (jnp.minimum(e, last), 0, 0)),
+                pl.BlockSpec((1, rhs, depth), lambda e, at, of: (e, 0, 0)),
+                pl.BlockSpec((1, 8, depth), lambda e, at, of: (e, 0, 0)),
+            ],
+            scratch_shapes=[VMEM((height, depth), F32)],
+        ),
+        out_shape=[
+            jax.ShapeDtypeStruct((count, height, depth), F32),
+            jax.ShapeDtypeStruct((steps, rhs, depth), F32),
+            jax.ShapeDtypeStruct((steps, 8, depth), F32),
+        ],
+        compiler_params=pltpu.CompilerParams(vmem_limit_bytes=VMEM_LIMIT),
+        name="apply_lower",
+    )(sources, targets, gathered, diag_inv, post, post)
+
+
+def remote(src, dst, send, recv, row, col):
+    return pltpu.make_async_remote_copy(
+        src_ref=src, dst_ref=dst, send_sem=send, recv_sem=recv, device_id=(row, col), device_id_type=MESH
+    )
+
+
+def redistribute(partial, post, lower_only):
+    count, rows, cols, share, width = partial.shape
+    tall = rows // CORES
+    full = cols * width
+    half = full // 2
+    with_post = post is not None
+
+    def kernel(*refs):
+        d, refs = refs[0], refs[1:]
+        if with_post:
+            piece, out, posted = refs[:3]
+            refs = refs[3:]
+        else:
+            out = refs[0]
+            refs = refs[1:]
+        give, own, one, two = refs[:4]
+        s1, r1, s2, r2, s3, r3, s4, r4, s5, r5, s6, r6 = refs[4:16]
+        row = lax.axis_index("row")
+        col = lax.axis_index("col")
+        core = row % CORES
+        y = row // CORES
+        mate = y * CORES + (1 - core)
+        across = (1 - y) * CORES + core
+        diagonal = (1 - y) * CORES + (1 - core)
+
+        def core_send(e):
+            return remote(d.at[e, :, 1 - core], one.at[e], s1.at[e], r1.at[e], mate, col)
+
+        def y_send(e):
+            return remote(give.at[e], two.at[e], s2.at[e], r2.at[e], across, col)
+
+        def col_send(e, step):
+            to = (col + step) % cols
+            return remote(
+                own.at[e, to],
+                out.at[e, row, :, pl.ds(pl.multiple_of(col * width, 128), width)],
+                s3.at[e, step - 1],
+                r3.at[e, step - 1],
+                row,
+                to,
+            )
+
+        def mate_send(e):
+            return remote(out.at[e, row], out.at[e, row], s4.at[e], r4.at[e], mate, col)
+
+        def upper(e, which):
+            return out.at[e, which, :, pl.ds(half, half)]
+
+        def across_full(e):
+            return remote(out.at[e, row], out.at[e, row], s5.at[e], r5.at[e], across, col)
+
+        def across_half(e):
+            return remote(upper(e, row), upper(e, row), s5.at[e], r5.at[e], across, col)
+
+        def forward_full(e):
+            return remote(out.at[e, across], out.at[e, across], s6.at[e], r6.at[e], mate, col)
+
+        def forward_half(e):
+            return remote(upper(e, across), upper(e, across), s6.at[e], r6.at[e], mate, col)
+
+        def loop(body):
+            def step(e, _):
+                body(e)
+                return 0
+
+            lax.fori_loop(0, count, step, 0)
+
+        loop(lambda e: core_send(e).start())
+
+        if with_post:
+            sp, rp = refs[16:18]
+
+            def post_send(step):
+                to_row = (row + step // cols) % rows
+                to_col = (col + step % cols) % cols
+                return remote(
+                    piece.at[to_col], posted.at[row, col], sp.at[step - 1], rp.at[step - 1], to_row, to_col
+                )
+
+            posted[row, col] = piece[col]
+
+            def post_start(step, _):
+                post_send(step).start()
+                return 0
+
+            lax.fori_loop(1, rows * cols, post_start, 0)
+
+        def send_cols(e):
+            for step in range(1, cols):
+                col_send(e, step).start()
+            out[e, row, :, pl.ds(pl.multiple_of(col * width, 128), width)] = own[e, col]
+
+        def first(e):
+            core_send(e).wait_recv()
+            if lower_only:
+
+                @pl.when(y == 0)
+                def _():
+                    give[e] = d[e, 1, core] + one[e, 1]
+                    y_send(e).start()
+                    own[e] = d[e, 0, core] + one[e, 0]
+                    send_cols(e)
+            else:
+                give[e] = d[e, 1 - y, core] + one[e, 1 - y]
+                y_send(e).start()
+
+        loop(first)
+
+        def second(e):
+            if lower_only:
+
+                @pl.when(y == 1)
+                def _():
+                    y_send(e).wait_recv()
+                    own[e] = d[e, 1, core] + (one[e, 1] + two[e])
+                    send_cols(e)
+            else:
+                y_send(e).wait_recv()
+                own[e] = d[e, y, core] + (one[e, y] + two[e])
+                send_cols(e)
+
+        loop(second)
+
+        def third(e):
+            for step in range(1, cols):
+                col_send(e, step).wait_recv()
+
+            @pl.when(y == 0)
+            def _():
+                across_half(e).start()
+
+            @pl.when(y == 1)
+            def _():
+                across_full(e).start()
+
+            mate_send(e).start()
+
+        loop(third)
+
+        def fourth(e):
+            @pl.when(y == 0)
+            def _():
+                across_full(e).wait_recv()
+                forward_full(e).start()
+
+            @pl.when(y == 1)
+            def _():
+                across_half(e).wait_recv()
+                forward_half(e).start()
+
+        loop(fourth)
+
+        def finish(e):
+            core_send(e).wait_send()
+            if lower_only:
+
+                @pl.when(y == 0)
+                def _():
+                    y_send(e).wait_send()
+            else:
+                y_send(e).wait_send()
+            for step in range(1, cols):
+                col_send(e, step).wait_send()
+            mate_send(e).wait()
+
+            @pl.when(y == 0)
+            def _():
+                across_half(e).wait_send()
+                forward_full(e).wait()
+
+            @pl.when(y == 1)
+            def _():
+                across_full(e).wait_send()
+                forward_half(e).wait()
+
+        loop(finish)
+
+        if with_post:
+
+            def post_wait(step, _):
+                post_send(step).wait()
+                return 0
+
+            lax.fori_loop(1, rows * cols, post_wait, 0)
+
+    spec = pl.BlockSpec(memory_space=VMEM)
+    dma = pltpu.SemaphoreType.DMA
+    out_shape = [jax.ShapeDtypeStruct((count, rows, share, full), F32)]
+    scratch = [
+        VMEM((count, cols, share, width), F32),
+        VMEM((count, cols, share, width), F32),
+        VMEM((count, tall, cols, share, width), F32),
+        VMEM((count, cols, share, width), F32),
+    ]
+    scratch += [dma((count,))] * 4 + [dma((count, cols - 1))] * 2 + [dma((count,))] * 6
+    args = [partial.reshape(count, tall, CORES, cols, share, width)]
+    if with_post:
+        out_shape.append(jax.ShapeDtypeStruct((rows,) + post.shape, F32))
+        scratch += [dma((rows * cols - 1,))] * 2
+        args.append(post)
+    return pl.pallas_call(
+        kernel,
+        out_shape=out_shape,
+        in_specs=[spec] * len(args),
+        out_specs=[spec] * len(out_shape),
+        scratch_shapes=scratch,
+        compiler_params=pltpu.CompilerParams(vmem_limit_bytes=VMEM_LIMIT, has_side_effects=True),
+        name="redistribute",
+    )(*args)
+
+
+def gather_cols(mine, cols):
+    count, height, depth = mine.shape
+    long = cols // WIDE
+    cut = height * 13 // 16 // 8 * 8
+    low, high = pl.ds(0, cut), pl.ds(cut, height - cut)
+
+    def kernel(own, out, up_s, up_r, down_s, down_r, x_s, x_r, b_s, b_r):
+        row = lax.axis_index("row")
+        col = lax.axis_index("col")
+        z = col // WIDE
+        x = col % WIDE
+        peer = z * WIDE + (1 - x)
+        spans = [(low, 0), (high, 0), (high, 1)]
+
+        def along(kind, hop, sign):
+            span, other = spans[kind]
+            block = (z - sign * hop) * WIDE + (x + other) % WIDE
+            ref = out.at[block, :, span]
+            sems = (up_s, up_r) if sign > 0 else (down_s, down_r)
+            return remote(ref, ref, sems[0].at[kind, hop], sems[1].at[kind, hop], row, (z + sign) * WIDE + x)
+
+        def sends(hop, sign):
+            return (z - hop >= 0) & (z + 1 < long) if sign > 0 else (z + hop < long) & (z >= 1)
+
+        def gets(hop, sign):
+            return z - 1 - hop >= 0 if sign > 0 else z + 1 + hop < long
+
+        def beside(offset):
+            block = ((z + offset + long) % long) * WIDE + x
+            ref = out.at[block, :, low]
+            return remote(ref, ref, x_s.at[offset], x_r.at[offset], row, peer)
+
+        def swap():
+            ref = out.at[col, :, high]
+            return remote(ref, ref, b_s.at[0], b_r.at[0], row, peer)
+
+        out[col] = own[...]
+        swap().start()
+        for sign in (1, -1):
+
+            @pl.when(sends(0, sign))
+            def _():
+                along(0, 0, sign).start()
+                along(1, 0, sign).start()
+
+        beside(0).start()
+        swap().wait_recv()
+        for sign in (1, -1):
+
+            @pl.when(sends(0, sign))
+            def _():
+                along(2, 0, sign).start()
+
+        for hop in range(long - 1):
+            for kind in range(3):
+                for sign in (1, -1):
+
+                    @pl.when(gets(hop, sign))
+                    def _():
+                        along(kind, hop, sign).wait_recv()
+
+                    if hop + 1 < long - 1:
+
+                        @pl.when(sends(hop + 1, sign))
+                        def _():
+                            along(kind, hop + 1, sign).start()
+
+                    if kind == 0:
+
+                        @pl.when(gets(hop, sign))
+                        def _():
+                            beside((long - sign * (hop + 1)) % long).start()
+
+        swap().wait_send()
+        for offset in range(long):
+            beside(offset).wait()
+        for hop in range(long - 1):
+            for kind in range(3):
+                for sign in (1, -1):
+
+                    @pl.when(sends(hop, sign))
+                    def _():
+                        along(kind, hop, sign).wait_send()
+
+    spec = pl.BlockSpec(memory_space=VMEM)
+    dma = pltpu.SemaphoreType.DMA
+    return pl.pallas_call(
+        kernel,
+        out_shape=jax.ShapeDtypeStruct((cols, count, height, depth), F32),
+        in_specs=[spec],
+        out_specs=spec,
+        scratch_shapes=[dma((3, long - 1))] * 4 + [dma((long,))] * 2 + [dma((1,))] * 2,
+        compiler_params=pltpu.CompilerParams(vmem_limit_bytes=VMEM_LIMIT, has_side_effects=True),
+        name="gather_cols",
+    )(mine)
+
+
+def scatter_sum(parts):
+    cols = parts.shape[0]
+
+    def kernel(src, out, landed, send, recv):
+        row = lax.axis_index("row")
+        col = lax.axis_index("col")
+
+        def copy(step):
+            to = (col + step) % cols
+            return remote(src.at[to], landed.at[step - 1], send.at[step - 1], recv.at[step - 1], row, to)
+
+        for step in range(1, cols):
+            copy(step).start()
+        total = src[col]
+        for step in range(1, cols):
+            copy(step).wait_recv()
+            total += landed[step - 1]
+        out[...] = total
+        for step in range(1, cols):
+            copy(step).wait_send()
+
+    spec = pl.BlockSpec(memory_space=VMEM)
+    dma = pltpu.SemaphoreType.DMA
+    return pl.pallas_call(
+        kernel,
+        out_shape=jax.ShapeDtypeStruct(parts.shape[1:], F32),
+        in_specs=[spec],
+        out_specs=spec,
+        scratch_shapes=[VMEM((cols - 1,) + parts.shape[1:], F32), dma((cols - 1,)), dma((cols - 1,))],
+        compiler_params=pltpu.CompilerParams(vmem_limit_bytes=VMEM_LIMIT, has_side_effects=True),
+        name="scatter_sum",
+    )(parts)
+
+
+def fast_body(rows, cols, factor, diag_inv, structure, parent, post):
+    supers, row_width, _, col_width = factor.shape
+    full = diag_inv.shape[1]
+    last = supers - 1
+    block_rows = row_width // structure.shape[2]
+    share = row_width // cols
+    height = rows * share
+    rhs_own = post.shape[2]
+    rhs = rhs_own * cols
+    far_count = supers - 2
+
+    extended = jnp.concatenate([parent, jnp.full((1,), supers, jnp.int32)])
+    first_at = parent
+    second_at = extended[parent]
+    first_clamped = jnp.minimum(first_at, last)
+    second_clamped = jnp.minimum(second_at, last)
+
+    def pick(s, target):
+        clamped = jnp.minimum(target, last)
+        block = lax.dynamic_index_in_dim(factor[:, :, s, :], clamped, 0, keepdims=False)
+        flags = lax.dynamic_index_in_dim(structure[s], clamped, 0, keepdims=False)
+        flags = jnp.where(target < supers, flags.astype(F32), 0.0)
+        return block * jnp.repeat(flags, block_rows)[:, None]
+
+    near_blocks = jnp.stack([pick(s, first_at[s]) for s in range(last)])
+    far_blocks = jnp.stack([pick(s, second_at[s]) for s in range(far_count)])
+
+    pieces = jnp.transpose(post.reshape(supers, cols, share, rhs_own), (1, 0, 3, 2))
+    pieces = pieces.reshape(cols, supers * rhs_own * share // 128, 128)
+
+    partial = near_partial(first_clamped[:last], diag_inv, near_blocks)
+    gathered, posted = redistribute(
+        partial.reshape(last, rows, cols, share, col_width), pieces, lower_only=True
+    )
+    posted = posted.reshape(rows, cols, supers, rhs_own, share)
+    posted = jnp.transpose(posted, (2, 1, 3, 0, 4)).reshape(supers, rhs, height)
+
+    order = jnp.arange(supers, dtype=jnp.int32)
+    near, means, squares = apply_lower(
+        order, first_clamped, gathered.reshape(last, height, full), diag_inv, posted, True, supers
+    )
+
+    children = jnp.any(parent[None, :] == order[:, None], axis=1)
+    middle = children & (parent < supers)
+    mid_low = jnp.argmax(middle).astype(jnp.int32)
+    mid_high = (last - jnp.argmax(middle[::-1])).astype(jnp.int32)
+    slots = (parent == mid_high).astype(jnp.int32)
+
+    def take(stacked, at):
+        return lax.dynamic_index_in_dim(stacked, jnp.minimum(at, last - 1), 0, keepdims=False)
+
+    chosen = jnp.stack([take(near, mid_low), take(near, mid_high)])
+    near_all = gather_cols(chosen, cols)
+
+    valid = (second_at < supers).astype(jnp.int32)
+    partial = far_partial(
+        slots[:far_count], second_clamped[:far_count], valid[:far_count], near_all, diag_inv,
+        near_blocks[:far_count], far_blocks,
+    )
+    (gathered,) = redistribute(partial.reshape(far_count, rows, cols, share, col_width), None, lower_only=False)
+    _, far_means, far_squares = apply_lower(
+        order[:far_count], second_clamped[:far_count], gathered.reshape(far_count, height, full), diag_inv,
+        posted, False, far_count,
+    )
+    means = means.at[:far_count].add(far_means)
+    squares = jnp.sum(squares.at[:far_count].add(far_squares), axis=1)
+
+    by_col = jnp.transpose(means.reshape(supers, cols, rhs_own, row_width), (1, 0, 2, 3))
+    by_col = by_col.reshape(cols, supers * rhs_own, row_width)
+    pad = -supers % 8
+    squares = jnp.concatenate([squares, jnp.zeros((pad, row_width), F32)], axis=0)
+    squares = jnp.broadcast_to(squares[None], (cols,) + squares.shape)
+    total = scatter_sum(jnp.concatenate([by_col, squares], axis=1))
+    mean_rows = supers * rhs_own
+    mean_x = jnp.swapaxes(total[:mean_rows].reshape(supers, rhs_own, row_width), 1, 2)
+    return mean_x, total[mean_rows : mean_rows + supers]
+
+
 def solution(mesh):
+    rows, cols = mesh.shape["row"], mesh.shape["col"]
+
+    def choose(factor, diag_inv, structure, parent, post):
+        shapes_fit = (
+            rows == 2 * CORES
+            and factor.shape[3] % 128 == 0
+            and factor.shape[1] % (8 * cols) == 0
+        )
+        if shapes_fit:
+            return fast_body(rows, cols, factor, diag_inv, structure, parent, post)
+        return body(factor, diag_inv, structure, parent, post)
+
     return jax.shard_map(
-        body,
+        choose,
         mesh=mesh,
         in_specs=(
             P(None, "row", None, "col"),

time: 1190 us -> 523 us (0.44)
  waiting for transfers between devices: 911 us -> 0 us
  Pallas kernels: 0 us -> 462 us
  matrix products: 143 us -> 0 us
  blocking collectives: 37.8 us -> 0 us
  other arithmetic: 36.9 us -> 22.4 us
  between operations: 27.8 us -> 13.5 us
    all_gather x5 -> x0, waiting for transfers between devices: 528 us -> none  [body(): blocks[current_sup] = lax.all_gather(mine, 'col', axis=1, tiled=True)]
    pallas_call x0 -> x8, Pallas kernels: none -> 462 us  [the longest x2 260 us: redistribute(): pl.pallas_call(kernel, out_shape=out_shape, in_specs=[spec] * len(args),...]
    psum x2 -> x0, waiting for transfers between devices: 383 us -> none  [solve(): summed = lax.psum(jnp.concatenate([unit_part, rhs_part], axis=0), 'row')]
    dot_general x31 -> x0, matrix products: 143 us -> none  [product(): jnp.dot(left, right, precision=HIGH, preferred_element_type=jnp.float32)]
    psum x1 -> x0, blocking collectives: 30.5 us -> none  [body(): variance = lax.psum(jnp.stack(squares), 'col')]
    concatenate x11 -> x2, other arithmetic: 16 us -> 1.74 us  [the longest x1 1.01 us: fast_body(): total = scatter_sum(jnp.concatenate([by_col, squares], axis=1))]
  transfers between devices with their start and end apart: 7 -> 0, of which waited for: 7 -> 0; matrix products, arithmetic and copies ran while one was open for 7% -> 0% of each run, Pallas kernels for 0% -> 0%
where the time goes in v1:
time: 523 us
  Pallas kernels  462 us (88%)
  local copies, waits for them, and re-layouts  24.5 us (5%)
  other arithmetic  22.4 us (4%)
  between operations  13.5 us (3%)
    pallas_call x2, Pallas kernels, redistribute(): pl.pallas_call(kernel, out_shape=out_shape, in_specs=[spec] * len(args),...  260 us
    pallas_call x1, Pallas kernels, gather_cols(): pl.pallas_call(kernel, out_shape=jax.ShapeDtypeStruct((cols, count, heigh...  89.8 us
    pallas_call x2, Pallas kernels, apply_lower(): pl.pallas_call(kernel, grid_spec=pltpu.PrefetchScalarGridSpec(num_scalar_...  39.7 us
    pallas_call x1, Pallas kernels, scatter_sum(): pl.pallas_call(kernel, out_shape=jax.ShapeDtypeStruct(parts.shape[1:], F3...  28.9 us
    pallas_call x1, Pallas kernels, far_partial(): pl.pallas_call(kernel, grid_spec=pltpu.PrefetchScalarGridSpec(num_scalar_...  25.5 us
    pallas_call x1, Pallas kernels, near_partial(): pl.pallas_call(kernel, grid_spec=pltpu.PrefetchScalarGridSpec(num_scalar_...  18.3 us
    slice x1, local copies, waits for them, and re-layouts, pick(): factor[:, :, s, :]  10.8 us

profile of v1, /device:TPU:10, one launch (start us, length us, event | category | flops | bytes accessed | tf_op | source)
XLA Modules:
  0.0 522.7 jit_solution(17311454054975858949)
XLA Ops:
  0.6 1.2 compare_select_fusion
  1.8 0.7 pad_add_fusion
  2.6 0.6 gather_fusion
  3.2 0.7 fusion.32
  4.5 1.5 fusion.31
  9.0 0.8 fusion.30
  9.8 0.2 fusion.19
  10.0 0.1 broadcast_bitcast_fusion.3
  10.1 0.1 broadcast_bitcast_fusion.8
  10.1 10.8 %fusion.29 = (f32[6,512,1,256]{3,1,2,0:T(8,128)}, f32[6,512,1,256]{3,1,2,0:T(8,128)}, f32[6,512,1,256]{3,1,2,0:T(8,128)}, f32[6,512,1,256]{3,1,2,0:T(8,128)}, f32[6,512,1,256]{3,1,2,0:T(8,128)S(1)}) fusion(f32[6,512,6,256]{3,1,2,0:T(8,128)} %param.9), kind=kLoop, calls=%fused_computation.86 | loop fusion | bytes 31457280 | tf_op jit(solution)/shard_map/slice | solution.py:639
  20.9 2.6 constant_dynamic-update-slice_fusion.3
  28.7 0.2 fusion.22
  29.0 0.1 broadcast_bitcast_fusion.2
  29.0 0.1 broadcast_bitcast_fusion.7
  29.1 2.6 constant_dynamic-update-slice_fusion.2
  31.7 0.1 broadcast_bitcast_fusion.1
  31.8 0.1 broadcast_bitcast_fusion.6
  31.8 2.5 constant_dynamic-update-slice_fusion.1
  35.6 0.0 copy-start.2
  35.6 0.0 copy-start.4
  35.6 0.0 copy-start.6
  36.9 0.2 fusion.28
  37.2 0.1 broadcast_bitcast_fusion
  37.2 1.0 constant_dynamic-update-slice_fusion
  38.2 0.0 copy-done.2
  38.3 0.0 copy-done.4
  38.3 0.0 copy-done.6
  38.3 1.6 pad_maximum_fusion.1.two
  39.8 0.0 copy-done.1
  39.8 0.0 copy-done.3
  39.8 0.4 copy-done.5
  40.3 1.5 pad_maximum_fusion.one
  41.8 0.1 broadcast_bitcast_fusion.4
  41.9 2.0 fusion.block
  43.9 18.3 %near_partial.1 = f32[5,2048,256]{2,1,0:T(8,128)} custom-call(s32[5]{0:T(128)} %bitcast.96, f32[6,2048,512]{2,1,0:T(8,128)} %lower.7, f32[5,512,256]{2,1,0:T(8,128)} %fusion.block), custom_call_target="tpu_custom_call" | custom-call | tf_op jit(solution)/shard_map/near_partial/pallas_call | solution.py:146
  62.2 0.1 reshape.552
  62.3 0.7 reshape.553.refs_1_
  63.1 138.1 %redistribute.2 = (f32[5,4,64,2048]{3,2,1,0:T(8,128)}, f32[4,8,24,128]{3,2,1,0:T(8,128)}) custom-call(f32[5,2,2,8,64,256]{5,4,3,2,1,0:T(8,128)} %bitcast.90, f32[8,24,128]{2,1,0:T(8,128)} %reshape.553.refs_1_), custom_call_target="tpu_custom_call" | custom-call | tf_op jit(solution)/shard_map/redistribute/pallas_call | solution.py:478
  201.2 1.2 reshape.555
  202.4 0.5 copy.19
  202.9 1.2 reshape.556.post_of.post_own
  204.1 0.5 iota.15.at
  204.6 22.4 %apply_lower.2 = (f32[5,256,512]{2,1,0:T(8,128)}, f32[6,64,512]{2,1,0:T(8,128)}, f32[6,8,512]{2,1,0:T(8,128)}) custom-call(s32[6]{0:T(128)} %iota.15.at, s32[6]{0:T(128)} %get-tuple-element.86.of, f32[5,256,2048]{2,1,0:T(8,128)} %bitcast.93, f32[6,2048,512]{2,1,0:T(8,128)} %lower.7, f32[6,64,256]{2,1,0:T(8,128)} %reshape.556.post_of.post_own, ...), custom_call_target="tpu_custom_call" | custom-call | tf_op jit(solution)/shard_map/apply_lower/pallas_call | solution.py:244
  227.1 0.1 fusion.1
  227.2 0.1 rev.3
  227.3 0.7 iota_reduce_fusion.1
  228.6 0.7 iota_reduce_fusion
  229.9 1.3 constant_dynamic-slice_fusion.5
  231.2 1.1 pad_maximum_fusion.2.own
  232.4 89.8 %gather_cols.1.near = f32[8,2,256,512]{3,2,1,0:T(8,128)} custom-call(f32[2,256,512]{2,1,0:T(8,128)} %pad_maximum_fusion.2.own), custom_call_target="tpu_custom_call" | custom-call | tf_op jit(solution)/shard_map/gather_cols/pallas_call | solution.py:575
  322.2 0.6 slice_convert_fusion
  322.7 0.5 broadcast_minimum_fusion
  323.3 25.5 %far_partial.1 = f32[4,2048,256]{2,1,0:T(8,128)} custom-call(s32[4]{0:T(128)} %get-tuple-element.93.slot, s32[4]{0:T(128)} %bitcast.97, s32[4]{0:T(128)} %get-tuple-element.92.ok, f32[8,2,256,512]{3,2,1,0:T(8,128)} %gather_cols.1.near, f32[6,2048,512]{2,1,0:T(8,128)} %lower.7, f32[4,512,256]{2,1,0:T(8,128)} %pad_maximum_fusion.one, ...), custom_call_target="tpu_custom_call" | custom-call | tf_op jit(solution)/shard_map/far_partial/pallas_call | solution.py:185
  348.8 121.8 %redistribute.3 = f32[4,4,64,2048]{3,2,1,0:T(8,128)} custom-call(f32[4,2,2,8,64,256]{5,4,3,2,1,0:T(8,128)} %bitcast.92), custom_call_target="tpu_custom_call" | custom-call | tf_op jit(solution)/shard_map/redistribute/pallas_call | solution.py:478
  470.6 0.5 iota.16
  471.1 17.3 %apply_lower.3 = (f32[4,256,512]{2,1,0:T(8,128)}, f32[4,64,512]{2,1,0:T(8,128)}, f32[4,8,512]{2,1,0:T(8,128)}) custom-call(s32[4]{0:T(128)} %bitcast.99, s32[4]{0:T(128)} %bitcast.98, f32[4,256,2048]{2,1,0:T(8,128)} %bitcast.91, f32[6,2048,512]{2,1,0:T(8,128)} %lower.7, f32[6,64,256]{2,1,0:T(8,128)} %reshape.556.post_of.post_own, ...), custom_call_target="tpu_custom_call" | custom-call | tf_op jit(solution)/shard_map/apply_lower/pallas_call | solution.py:244
  488.5 1.2 add_dynamic-update-slice_fusion
  489.7 0.1 copy_bitcast_fusion
  489.7 0.0 copy-done.7
  489.8 0.0 copy-done.9
  489.9 1.0 pad_maximum_fusion.3.src
  490.9 28.9 %scatter_sum.1 = f32[56,512]{1,0:T(8,128)} custom-call(f32[8,56,512]{2,1,0:T(8,128)} %pad_maximum_fusion.3.src), custom_call_target="tpu_custom_call" | custom-call | tf_op jit(solution)/shard_map/scatter_sum/pallas_call | solution.py:609
  519.8 1.5 slice_bitcast_fusion
  521.4 1.3 slice.170
  (20 shorter events, 0.1 us)
Async XLA Ops:
  35.6 2.7 copy-start.2
  35.6 2.7 copy-start.4
  35.6 2.7 copy-start.6
  38.2 1.6 copy-start.1
  38.2 1.6 copy-start.3
  38.2 2.0 copy-start.5
  43.9 18.3 %copy-start.8 = (f32[6,512,8]{1,2,0:T(8,128)S(1)}, f32[6,512,8]{1,2,0:T(8,128)}, u32[]{:S(2)}) copy-start(f32[6,512,8]{1,2,0:T(8,128)} %param.13) | copy-start | bytes 294916
  204.6 22.4 %copy-start.10 = (s32[6]{0:T(128)S(1)}, s32[6]{0:T(128)}, u32[]{:S(2)}) copy-start(s32[6]{0:T(128)} %param.12) | copy-start | bytes 76
  471.1 17.3 %copy-start = (f32[6,64,512]{2,1,0:T(8,128)S(1)}, f32[6,64,512]{2,1,0:T(8,128)}, u32[]{:S(2)}) copy-start(f32[6,64,512]{2,1,0:T(8,128)} %get-tuple-element.37) | copy-start | bytes 2359300
  488.4 1.3 copy-start.7
  488.4 1.3 copy-start.9
